TPU v7x, 32 devices: a whole 2x2x4 slice. The times are simulated.
32 devices in a mesh: doc: 2 (over x), seq: 4 (over y, core), head: 4 (over z).
Axes of the slice: x: 2, y: 2, z: 4, core: 2. Of those that a mesh axis runs over, the one named last changes fastest.
Arguments:
- length: int32 [2], P('doc'), parts along dimension 0, may hold values from 896 to 1024
- residual: bfloat16 [2048, 4096], P(('doc', 'seq'), 'head'), parts along dimension 0, may hold values from -6 to 6
- ssm_input: bfloat16 [2048, 4096], P(('doc', 'seq'), 'head'), parts along dimension 0, may hold values from -6 to 6
- state_in: bfloat16 [2048, 128], P(('doc', 'seq')), parts along dimension 0, may hold values from -6 to 6
- state_out: bfloat16 [2048, 128], P(('doc', 'seq')), parts along dimension 0, may hold values from -0.5 to 0.5
- step_raw: float32 [128, 1024], P(('doc', 'head'), 'seq'), parts along dimension 0, may hold values from -5 to 2
- decay_rate: float32 [64], P('head'), may hold values from 0 to 1, as said below
- ssm_gain: float32 [4096], P('head'), may hold values from 0.1 to 1.9
- out_weight: bfloat16 [4096, 4096], P('head'), may hold values from -0.09375 to 0.09375
- norm_gain: float32 [4096], replicated, may hold values from 0.1 to 1.9
- query_weight: bfloat16 [4096, 4096], P(None, 'head'), may hold values from -2 to 2
- key_weight: bfloat16 [4096, 1024], P(None, 'head'), may hold values from -3 to 3
- value_weight: bfloat16 [4096, 1024], P(None, 'head'), may hold values from -0.09375 to 0.09375
Outputs:
- layer_out: bfloat16 [2048, 4096], P(('doc', 'seq'), 'head'), parts along dimension 0
- head_out: bfloat16 [2048, 4096], P(('doc', 'seq'), 'head'), parts along dimension 0
There are 2 independent parts, one for each index of `doc`. A program takes and returns all parts, laid end to end along the dimension named above; an argument that names none is the same for every part. Nothing has to cross between parts.
Inputs may be any that keep to these rules, and one draw needn't show every extreme that they name: The document fills positions 0 to length - 1 of the 1024; later positions are padding. `decay_rate`: positive.
All inputs are finite; a program needn't handle non-finite values.
Results may differ from a plain program's by a relative error of at most 0.028.
The roundings to bfloat16 on the way count: a program that leaves them out, or rounds other values in their place, can miss the bound.
Values may be sent and summed in bfloat16 or wider, within the bound.
A program may use at most 64 MiB of HBM per device.

v0:
```python
import jax
import jax.numpy as jnp
from jax import lax
from jax.sharding import PartitionSpec as P

HEAD_DIM = 128
EPSILON = 1e-05
NEG_BIG = -1e30
HIGHEST = lax.Precision.HIGHEST


def prefix_2(value, axis, join, neutral):
    count, mine = (lax.axis_size(axis), lax.axis_index(axis))
    pieces = jax.tree.map(lambda part: lax.all_gather(part, axis), value)
    so_far = jax.tree.map(
        lambda part, zero: jnp.full_like(part, 0) + jnp.asarray(zero, part.dtype), value, neutral
    )

    def turn(position, so_far):
        longer = join(so_far, jax.tree.map(lambda part: part[position], pieces))
        return jax.tree.map(lambda new, old: jnp.where(position < mine, new, old), longer, so_far)

    return lax.fori_loop(0, count - 1, turn, so_far)


def chain_link(earlier, later):
    return (earlier[0] * later[0], later[0][:, None, None] * earlier[1] + later[1])


def body(
    length,
    residual,
    ssm_input,
    state_in,
    state_out,
    step_raw,
    decay_rate,
    ssm_gain,
    out_weight,
    norm_gain,
    query_weight,
    key_weight,
    value_weight,
):
    rows = residual.shape[0]
    local_heads = decay_rate.shape[0]
    head_width = ssm_input.shape[1] // local_heads
    seq_index = lax.axis_index("seq")
    limit = length[0]
    positions = seq_index * rows + jnp.arange(rows, dtype=jnp.int32)
    live_rows = positions < limit
    live = live_rows.astype(jnp.float32)
    delta = live[None, :] * jax.nn.softplus(step_raw)
    cumlog = jnp.cumsum(-decay_rate[:, None] * delta, axis=1)
    inputs = ssm_input.astype(jnp.float32).reshape(rows, local_heads, head_width)
    inner = jnp.dot(state_out, state_in.T, preferred_element_type=jnp.float32)
    causal = jnp.arange(rows)[:, None] >= jnp.arange(rows)[None, :]
    spread = cumlog[:, :, None] - cumlog[:, None, :]
    mixing = (
        jnp.where(causal[None], jnp.exp(jnp.where(causal[None], spread, 0.0)), 0.0)
        * inner[None]
        * delta[:, None, :]
    )
    within = jnp.einsum("hts,shp->thp", mixing, inputs, precision=HIGHEST)
    tail = jnp.exp(cumlog[:, -1:] - cumlog) * delta
    local_state = jnp.einsum(
        "hs,shp,sn->hpn", tail, inputs, state_in.astype(jnp.float32), precision=HIGHEST
    )
    block_decay = jnp.exp(cumlog[:, -1])
    prefix = prefix_2(
        (block_decay, local_state),
        "seq",
        chain_link,
        (jnp.ones_like(block_decay), jnp.zeros_like(local_state)),
    )
    incoming = prefix[1]
    carried = jnp.einsum("hpn,tn->thp", incoming, state_out.astype(jnp.float32), precision=HIGHEST)
    ssm_out = (within + jnp.exp(cumlog).T[:, :, None] * carried) * live[:, None, None]
    mean_square = jnp.mean(ssm_out * ssm_out, axis=2, keepdims=True)
    normed = (
        ssm_out * lax.rsqrt(mean_square + EPSILON) * ssm_gain.reshape(local_heads, head_width)
    ).astype(jnp.bfloat16)
    normed = normed.reshape(rows, local_heads * head_width)
    partial_value = jnp.dot(normed, out_weight, preferred_element_type=jnp.float32)
    model_width = norm_gain.shape[0]
    own_width = residual.shape[1]
    projected = lax.psum_scatter(partial_value, "head", scatter_dimension=1, tiled=True)
    layer_out = (residual.astype(jnp.float32) + projected).astype(jnp.bfloat16)
    widened = layer_out.astype(jnp.float32)
    squares = lax.psum(jnp.sum(widened * widened, axis=1), "head")
    piece_gain = lax.dynamic_slice_in_dim(norm_gain, lax.axis_index("head") * own_width, own_width)
    scaled = (widened * lax.rsqrt(squares / model_width + EPSILON)[:, None] * piece_gain).astype(
        jnp.bfloat16
    )
    attn_in = lax.all_gather(scaled, "head", axis=1, tiled=True)
    queries = jnp.dot(attn_in, query_weight, preferred_element_type=jnp.float32).astype(
        jnp.bfloat16
    )
    keys = jnp.dot(attn_in, key_weight, preferred_element_type=jnp.float32).astype(jnp.bfloat16)
    values = jnp.dot(attn_in, value_weight, preferred_element_type=jnp.float32).astype(jnp.bfloat16)
    query_local = query_weight.shape[1] // HEAD_DIM
    kv_local = key_weight.shape[1] // HEAD_DIM
    group_size = query_local // kv_local
    grouped = queries.reshape(rows, kv_local, group_size, HEAD_DIM)
    best = jnp.full((rows, query_local), NEG_BIG, jnp.float32)
    key_piece = lax.all_gather(keys, "seq", axis=0, tiled=True)
    value_piece = lax.all_gather(values, "seq", axis=0, tiled=True)
    count = key_piece.shape[0]
    key_pos = jnp.arange(count, dtype=jnp.int32)
    allowed = (key_pos[None, :] <= positions[:, None]) & (key_pos[None, :] < limit)
    scores = jnp.einsum(
        "tkgd,rkd->tkgr",
        grouped,
        key_piece.reshape(count, kv_local, HEAD_DIM),
        preferred_element_type=jnp.float32,
    ) * HEAD_DIM ** (-0.5)
    scores = scores.reshape(rows, query_local, count)
    allowed_wide = allowed[:, None, :]
    masked = jnp.where(allowed_wide, scores, NEG_BIG)
    new_best = jnp.maximum(best, jnp.max(masked, axis=2))
    weights = jnp.where(allowed_wide, jnp.exp(masked - new_best[:, :, None]), 0.0)
    total = jnp.sum(weights, axis=2)
    update = jnp.einsum(
        "tkgr,rkd->tkgd",
        weights.astype(jnp.bfloat16).reshape(rows, kv_local, group_size, count),
        value_piece.reshape(count, kv_local, HEAD_DIM),
        preferred_element_type=jnp.float32,
    )
    accum = update.reshape(rows, query_local, HEAD_DIM)
    folded = (new_best, total, accum)
    total = folded[1]
    accum = folded[2]
    safe_total = jnp.where(live_rows[:, None], total, 1.0)
    head_out = (
        (accum / safe_total[:, :, None] * live[:, None, None])
        .astype(jnp.bfloat16)
        .reshape(rows, query_local * HEAD_DIM)
    )
    return (layer_out, head_out)


def solution(mesh):
    placed = (
        P("doc"),
        P(("doc", "seq"), "head"),
        P(("doc", "seq"), "head"),
        P(("doc", "seq"), None),
        P(("doc", "seq"), None),
        P(("doc", "head"), "seq"),
        P("head"),
        P("head"),
        P("head", None),
        P(),
        P(None, "head"),
        P(None, "head"),
        P(None, "head"),
    )
    return jax.shard_map(
        body,
        mesh=mesh,
        in_specs=placed,
        out_specs=(P(("doc", "seq"), "head"), P(("doc", "seq"), "head")),
        check_vma=False,
    )
```

profile of v0, /device:TPU:0, one launch (start us, length us, event | category | flops | bytes accessed | tf_op | source)
XLA Modules:
  0.0 233.8 jit_solution(13353778681474807331)
XLA Ops:
  8.0 0.7 neg.8
  8.7 0.8 multiply_bitcast_fusion.1
  9.5 0.6 reduce-window.6
  10.0 0.2 slice_reduce_fusion
  10.2 0.1 copy_bitcast_fusion
  10.3 0.2 slice_reduce_fusion.1
  10.5 1.2 copy.34
  11.8 0.1 exponential_bitcast_fusion
  11.9 2.3 fusion.31
  14.2 0.0 reduce-scatter.2.cloned.1.call-start
  14.2 0.8 mul.159
  15.0 1.2 dynamic-slice
  16.9 0.2 dynamic-update-slice
  17.1 8.4 %all-reduce = f32[64]{0:T(128)S(1)} all-reduce(f32[64]{0:T(128)S(1)} %dynamic-update-slice), channel_id=2, replica_groups=mesh['doc'=2,'seq'=4,'head'=4] {'seq'}, use_global_device_ids=true, to_apply=%add | all-reduce | flops 64 | bytes 512
  25.5 0.1 reshape.196
  25.6 1.1 fusion.48
  26.7 4.4 %fusion.20 = f32[256,16,64]{0,2,1:T(8,128)} fusion(bf16[256,16,64]{0,2,1:T(8,128)(2,1)S(1)} %bitcast.100, f32[16,256]{1,0:T(8,128)S(1)} %get-tuple-element.130, f32[256,256]{1,0:T(8,128)S(1)} %fusion.48, f32[16,256]{1,0:T(8,128)S(1)} %copy_bitcast_fusion, pred[256,256]{1,0:T(8,128)(4,1)S(1)} %iota_compare_fusion.1), kind=kOutput, calls=%fused_computation.24 | convolution fusion | flops 810549248 | bytes 1933312 | tf_op jit(solution)/shard_map/hts,shp->thp/dot_general | solution.py:64
  31.1 8.5 %all-gather.7.cloned.1.call-done = f32[64,64,128]{2,1,0:T(8,128)} async-done(((f32[16,64,128]{2,1,0:T(8,128)}), f32[64,64,128]{2,1,0:T(8,128)}) %all-gather.7.cloned.1.call-update) | async-done | bytes 2097168 | tf_op jit(solution)/shard_map/all_gather | solution.py:14
  39.6 3.6 %while.14 = (s32[]{:T(128)}, f32[16,64,128]{2,1,0:T(8,128)S(1)}, s32[]{:T(128)}, f32[4,16]{1,0:T(4,128)S(1)}, f32[4,16,64,128]{3,2,1,0:T(8,128)}, /*index=5*/s32[]{:T(128)}, s32[]{:T(128)}) while((s32[]{:T(128)}, f32[16,64,128]{2,1,0:T(8,128)S(1)}, s32[]{:T(128)}, f32[4,16]{1,0:T(4,128)S(1)}, f32[4,16,64,128]{3,2,1,0:T(8,128)}, ...), condition=%wide.region_3.4_spmd.clone, body=%wide.region_2.3_spmd.clone.sunk | while | flops 524292 | bytes 1573169 | solution.py:23
  39.6 1.2 fusion.64
  40.8 1.2 fusion.64
  42.1 1.2 fusion.64
  43.2 1.9 multiply_reduce_fusion
  45.1 0.2 multiply_convert_fusion
  45.4 7.7 %fusion.49 = f32[256,4096]{1,0:T(8,128)} fusion(bf16[256,1024]{0,1:T(8,128)(2,1)S(1)} %bitcast.98, bf16[1024,4096]{1,0:T(8,128)(2,1)} %param.23), kind=kOutput, calls=%fused_computation.78 | convolution fusion | flops 2147483648 | bytes 13107200 | tf_op jit(solution)/shard_map/dot_general | solution.py:84
  53.1 0.0 all-gather.5.cloned.1.call-start
  53.1 0.7 dynamic_slice.17
  53.9 76.2 %reduce-scatter.2.cloned.1.call-done = f32[256,1024]{1,0:T(8,128)} async-done(((f32[256,4096]{1,0:T(8,128)}), f32[256,1024]{1,0:T(8,128)}) %reduce-scatter.2.cloned.1.call-update) | async-done | bytes 1048592 | tf_op jit(solution)/shard_map/reduce_scatter | solution.py:87
  130.0 1.5 fusion.26
  131.5 11.0 %psum.7 = f32[256]{0:T(256)S(1)} all-reduce(f32[256]{0:T(256)S(1)} %get-tuple-element.127), channel_id=1, replica_groups=mesh['doc'=2,'seq'=4,'head'=4] {'head'}, use_global_device_ids=true, to_apply=%region_7.8 | all-reduce | flops 256 | bytes 2048 | tf_op jit(solution)/shard_map/psum | solution.py:90
  142.5 1.0 fusion.28
  143.5 0.2 fusion.34
  143.8 43.9 %all-gather.5.cloned.1.call-done = bf16[256,4096]{1,0:T(8,128)(2,1)} async-done(((bf16[256,1024]{1,0:T(8,128)(2,1)}), bf16[256,4096]{1,0:T(8,128)(2,1)}) %all-gather.5.cloned.1.call-update) | async-done | bytes 2097168 | tf_op jit(solution)/shard_map/all_gather | solution.py:95
  187.7 6.3 %convolution_convert_fusion = bf16[256,1024]{1,0:T(8,128)(2,1)S(1)} fusion(bf16[256,4096]{1,0:T(8,128)(2,1)} %all-gather.5.cloned.1.call-done, bf16[4096,1024]{1,0:T(8,128)(2,1)} %param.25), kind=kOutput, calls=%fused_computation.30 | convolution fusion | flops 2147745792 | bytes 11010048 | tf_op jit(solution)/shard_map/dot_general | solution.py:96
  194.0 1.2 reshape.194
  195.2 2.3 convolution_convert_fusion.2
  197.5 7.2 %all_gather.23 = bf16[1024,256]{1,0:T(8,128)(2,1)S(1)} all-gather(bf16[256,256]{1,0:T(8,128)(2,1)S(1)} %convolution_convert_fusion.2), channel_id=1, replica_groups=mesh['doc'=2,'seq'=4,'head'=4] {'seq'}, dimensions={0}, use_global_device_ids=true | all-gather | bytes 655360 | tf_op jit(solution)/shard_map/all_gather | solution.py:107
  204.6 0.2 copy.44
  204.9 2.9 %convolution_convert_fusion.1 = bf16[256,256]{1,0:T(8,128)(2,1)S(1)} fusion(bf16[256,4096]{1,0:T(8,128)(2,1)} %all-gather.5.cloned.1.call-done, bf16[4096,256]{1,0:T(8,128)(2,1)} %param.26), kind=kOutput, calls=%fused_computation.31 | convolution fusion | flops 536936448 | bytes 4325376 | tf_op jit(solution)/shard_map/dot_general | solution.py:99
  207.8 7.5 %all_gather.24 = bf16[1024,256]{1,0:T(8,128)(2,1)S(1)} all-gather(bf16[256,256]{1,0:T(8,128)(2,1)S(1)} %convolution_convert_fusion.1), channel_id=1, replica_groups=mesh['doc'=2,'seq'=4,'head'=4] {'seq'}, dimensions={0}, use_global_device_ids=true | all-gather | bytes 655360 | tf_op jit(solution)/shard_map/all_gather | solution.py:106
  215.3 0.9 reshape.193
  216.2 2.7 %fusion.1 = (f32[256,2,4]{0,2,1:T(4,128)S(1)}, f32[2,1024,256,4]{2,1,3,0:T(8,128)S(1)}) fusion(pred[256,1024]{0,1:T(8,128)(4,1)S(1)} %fusion.34, bf16[256,2,4,128]{3,2,1,0:T(4,128)(2,1)} %reshape.194, bf16[1024,2,128,1]{2,1,0,3:T(2,128)(2,1)} %bitcast.103), kind=kOutput, calls=%fused_computation.5 | convolution fusion | flops 543160320 | bytes 9707520 | tf_op jit(solution)/shard_map/tkgd,rkd->tkgr/dot_general | solution.py:111
  218.9 2.0 fusion.2
  220.9 3.2 %fusion.11 = f32[2,128,256,4]{2,1,3,0:T(8,128)} fusion(bf16[1024,2,128,1]{0,2,3,1:T(8,128)(2,1)S(1)} %bitcast.102, f32[2,1024,256,4]{2,1,3,0:T(8,128)S(1)} %get-tuple-element.138, f32[256,2,4]{0,2,1:T(4,128)S(1)} %broadcast_maximum_fusion, pred[256,1024]{0,1:T(8,128)(4,1)S(1)} %fusion.34), kind=kOutput, calls=%fused_computation.15 | convolution fusion | flops 547356672 | bytes 10231808 | tf_op jit(solution)/shard_map/tkgr,rkd->tkgd/dot_general | solution.py:123
  224.1 1.6 copy.40
  225.7 0.1 copy.39
  225.9 0.3 div.27
  226.2 1.0 fusion.30
  (29 shorter events, 0.3 us)
Async XLA Ops:
  7.2 188.0 %copy-start = (bf16[4096,256]{1,0:T(8,128)(2,1)S(1)}, bf16[4096,256]{1,0:T(8,128)(2,1)}, u32[]{:S(2)}) copy-start(bf16[4096,256]{1,0:T(8,128)(2,1)} %param.27) | copy-start | bytes 6291460
  7.2 32.4 %all-gather.7.cloned.1.call-start = ((), (), s32[]{:S(2)}) async-start(), calls=%async_computation.3 | async-start | bytes 2621440 | tf_op jit(solution)/shard_map/all_gather | solution.py:14
  14.2 115.8 %reduce-scatter.2.cloned.1.call-start = ((), (), s32[]{:S(2)}) async-start(), calls=%async_computation.1 | async-start | bytes 5242880 | tf_op jit(solution)/shard_map/reduce_scatter | solution.py:87
  31.1 12.2 %copy-start.3 = (bf16[256,128]{1,0:T(8,128)(2,1)S(1)}, bf16[256,128]{1,0:T(8,128)(2,1)}, u32[]{:S(2)}) copy-start(bf16[256,128]{1,0:T(8,128)(2,1)} %param.19) | copy-start | bytes 196612
  53.0 77.0 %copy-start.2 = (bf16[256,1024]{1,0:T(8,128)(2,1)S(1)}, bf16[256,1024]{1,0:T(8,128)(2,1)}, u32[]{:S(2)}) copy-start(bf16[256,1024]{1,0:T(8,128)(2,1)} %param.16) | copy-start | bytes 1572868
  53.1 134.6 %all-gather.5.cloned.1.call-start = ((), (), s32[]{:S(2)}) async-start(), calls=%async_computation.2 | async-start | bytes 2621440 | tf_op jit(solution)/shard_map/all_gather | solution.py:95
  131.5 62.5 %copy-start.1 = (bf16[256,1024]{1,0:T(8,128)(2,1)}, bf16[256,1024]{1,0:T(8,128)(2,1)S(1)}, u32[]{:S(2)}) copy-start(bf16[256,1024]{1,0:T(8,128)(2,1)S(1)} %get-tuple-element.128) | copy-start | bytes 1572868
Sparse Core Ops, SparseCore 0:
  14.3 25.2 all-gather.6
  53.2 76.7 reduce-scatter.1
  143.6 43.9 all-gather.4
where the time goes:
time: 235 us; the launch traced here: 234 us
  waiting for transfers between devices  129 us (55%)
  matrix products  34.8 us (15%)
  blocking collectives  34 us (14%)
  between operations  15.4 us (7%)
  other arithmetic  11.7 us (5%)
  local copies, waits for them, and re-layouts  9.02 us (4%)
    reduce_scatter x1, waiting for transfers between devices, body(): lax.psum_scatter(partial_value, 'head', scatter_dimension=1, tiled=True)  76.2 us
    all_gather x1, waiting for transfers between devices, body(): attn_in = lax.all_gather(scaled, 'head', axis=1, tiled=True)  43.9 us
    psum x1, blocking collectives, body(): squares = lax.psum(jnp.sum(widened * widened, axis=1), 'head')  11 us
    all_gather x1, waiting for transfers between devices, prefix_2(): pieces = jax.tree.map(lambda part: lax.all_gather(part, axis), value)  8.54 us
    unnamed x1, blocking collectives  8.37 us
    dot_general x1, matrix products, body(): jnp.dot(normed, out_weight, preferred_element_type=jnp.float32)  7.69 us
    all_gather x1, blocking collectives, body(): key_piece = lax.all_gather(keys, 'seq', axis=0, tiled=True)  7.46 us
    all_gather x1, blocking collectives, body(): value_piece = lax.all_gather(values, 'seq', axis=0, tiled=True)  7.15 us
  transfers between devices with their start and end apart: 3, of which 3 were waited for; matrix products, arithmetic and copies ran while one was open for 4% of the time, Pallas kernels for 0%

commit v1 on v0

--- a/solution.py
+++ b/solution.py
@@ -92,7 +92,7 @@
     scaled = (widened * lax.rsqrt(squares / model_width + EPSILON)[:, None] * piece_gain).astype(
         jnp.bfloat16
     )
-    attn_in = lax.all_gather(scaled, "head", axis=1, tiled=True)
+    attn_in = jnp.concatenate(lax.all_gather(scaled, "head"), axis=1)
     queries = jnp.dot(attn_in, query_weight, preferred_element_type=jnp.float32).astype(
         jnp.bfloat16
     )

time: 235 us -> 236 us (level)
  local copies, waits for them, and re-layouts: 9.02 us -> 13.3 us
  matrix products: 34.8 us -> 32.3 us
    all_gather x0 -> x1, local copies, waits for them, and re-layouts: none -> 3.93 us  [body(): attn_in = jnp.concatenate(lax.all_gather(scaled, 'head'), axis=1)]
where the time goes in v1:
time: 236 us; the launch traced here: 235 us
  waiting for transfers between devices  129 us (55%)
  blocking collectives  34 us (14%)
  matrix products  32.3 us (14%)
  between operations  15.4 us (7%)
  local copies, waits for them, and re-layouts  13.3 us (6%)
  other arithmetic  11.7 us (5%)
    reduce_scatter x1, waiting for transfers between devices, body(): lax.psum_scatter(partial_value, 'head', scatter_dimension=1, tiled=True)  76.2 us
    all_gather x1, waiting for transfers between devices, body(): attn_in = jnp.concatenate(lax.all_gather(scaled, 'head'), axis=1)  43.9 us
    psum x1, blocking collectives, body(): squares = lax.psum(jnp.sum(widened * widened, axis=1), 'head')  11 us
    all_gather x1, waiting for transfers between devices, prefix_2(): pieces = jax.tree.map(lambda part: lax.all_gather(part, axis), value)  8.54 us
    unnamed x1, blocking collectives  8.37 us
    dot_general x1, matrix products, body(): jnp.dot(normed, out_weight, preferred_element_type=jnp.float32)  7.69 us
    all_gather x1, blocking collectives, body(): key_piece = lax.all_gather(keys, 'seq', axis=0, tiled=True)  7.46 us
    all_gather x1, blocking collectives, body(): value_piece = lax.all_gather(values, 'seq', axis=0, tiled=True)  7.14 us
  transfers between devices with their start and end apart: 3, of which 3 were waited for; matrix products, arithmetic and copies ran while one was open for 4% of the time, Pallas kernels for 0%

profile of v1, /device:TPU:0, one launch (start us, length us, event | category | flops | bytes accessed | tf_op | source)
XLA Modules:
  0.0 235.5 jit_solution(16810915453964323800)
XLA Ops:
  8.0 0.7 neg.8
  8.7 0.8 multiply_bitcast_fusion.1
  9.5 0.6 reduce-window.6
  10.0 0.2 slice_reduce_fusion
  10.2 0.1 copy_bitcast_fusion
  10.3 0.2 slice_reduce_fusion.1
  10.5 1.2 copy.35
  11.8 0.1 exponential_bitcast_fusion
  11.9 2.3 fusion.31
  14.2 0.8 mul.159
  15.0 1.2 dynamic-slice
  16.9 0.2 dynamic-update-slice
  17.1 8.4 %all-reduce = f32[64]{0:T(128)S(1)} all-reduce(f32[64]{0:T(128)S(1)} %dynamic-update-slice), channel_id=2, replica_groups=mesh['doc'=2,'seq'=4,'head'=4] {'seq'}, use_global_device_ids=true, to_apply=%add | all-reduce | flops 64 | bytes 512
  25.5 0.1 reshape.204
  25.6 1.1 fusion.48
  26.7 4.4 %fusion.20 = f32[256,16,64]{0,2,1:T(8,128)} fusion(bf16[256,16,64]{0,2,1:T(8,128)(2,1)S(1)} %bitcast.108, f32[16,256]{1,0:T(8,128)S(1)} %get-tuple-element.130, f32[256,256]{1,0:T(8,128)S(1)} %fusion.48, f32[16,256]{1,0:T(8,128)S(1)} %copy_bitcast_fusion, pred[256,256]{1,0:T(8,128)(4,1)S(1)} %iota_compare_fusion.1), kind=kOutput, calls=%fused_computation.24 | convolution fusion | flops 810549248 | bytes 1933312 | tf_op jit(solution)/shard_map/hts,shp->thp/dot_general | solution.py:64
  31.1 8.5 %all-gather.6.cloned.1.call-done = f32[64,64,128]{2,1,0:T(8,128)} async-done(((f32[16,64,128]{2,1,0:T(8,128)}), f32[64,64,128]{2,1,0:T(8,128)}) %all-gather.6.cloned.1.call-update) | async-done | bytes 2097168 | tf_op jit(solution)/shard_map/all_gather | solution.py:14
  39.6 3.6 %while.14 = (s32[]{:T(128)}, f32[16,64,128]{2,1,0:T(8,128)S(1)}, s32[]{:T(128)}, f32[4,16]{1,0:T(4,128)S(1)}, f32[4,16,64,128]{3,2,1,0:T(8,128)}, /*index=5*/s32[]{:T(128)}, s32[]{:T(128)}) while((s32[]{:T(128)}, f32[16,64,128]{2,1,0:T(8,128)S(1)}, s32[]{:T(128)}, f32[4,16]{1,0:T(4,128)S(1)}, f32[4,16,64,128]{3,2,1,0:T(8,128)}, ...), condition=%wide.region_3.4_spmd.clone, body=%wide.region_2.3_spmd.clone.sunk | while | flops 524292 | bytes 1573169 | solution.py:23
  39.6 1.2 fusion.64
  40.8 1.2 fusion.64
  42.1 1.2 fusion.64
  43.2 1.9 multiply_reduce_fusion
  45.1 0.2 multiply_convert_fusion
  45.3 7.7 %fusion.49 = f32[256,4096]{1,0:T(8,128)} fusion(bf16[256,1024]{0,1:T(8,128)(2,1)S(1)} %bitcast.105, bf16[1024,4096]{1,0:T(8,128)(2,1)} %param.23), kind=kOutput, calls=%fused_computation.78 | convolution fusion | flops 2147483648 | bytes 13107200 | tf_op jit(solution)/shard_map/dot_general | solution.py:84
  53.1 0.7 dynamic_slice.17
  53.9 76.2 %reduce-scatter.2.cloned.1.call-done = f32[256,1024]{1,0:T(8,128)} async-done(((f32[256,4096]{1,0:T(8,128)}), f32[256,1024]{1,0:T(8,128)}) %reduce-scatter.2.cloned.1.call-update) | async-done | bytes 1048592 | tf_op jit(solution)/shard_map/reduce_scatter | solution.py:87
  130.0 1.5 fusion.26
  131.5 11.0 %psum.7 = f32[256]{0:T(256)S(1)} all-reduce(f32[256]{0:T(256)S(1)} %get-tuple-element.127), channel_id=1, replica_groups=mesh['doc'=2,'seq'=4,'head'=4] {'head'}, use_global_device_ids=true, to_apply=%region_7.8 | all-reduce | flops 256 | bytes 2048 | tf_op jit(solution)/shard_map/psum | solution.py:90
  142.5 1.0 fusion.28
  143.5 0.2 fusion.34
  143.8 43.9 %all-gather.8.cloned.1.call-done = bf16[1024,1024]{1,0:T(8,128)(2,1)} async-done(((bf16[256,1024]{1,0:T(8,128)(2,1)}), bf16[1024,1024]{1,0:T(8,128)(2,1)}) %all-gather.8.cloned.1.call-update) | async-done | bytes 2097168 | tf_op jit(solution)/shard_map/all_gather | solution.py:95
  187.7 3.9 %copy.36 = bf16[4,256,1024]{1,2,0:T(8,128)(2,1)} copy(bf16[4,256,1024]{2,1,0:T(8,128)(2,1)} %bitcast.106) | data formatting | bytes 4194304 | tf_op jit(solution)/shard_map/all_gather | solution.py:95
  191.6 2.5 %convolution_convert_fusion.1 = bf16[256,256]{1,0:T(8,128)(2,1)S(1)} fusion(bf16[256,4096]{0,1:T(8,128)(2,1)} %bitcast.100, bf16[4096,256]{1,0:T(8,128)(2,1)S(1)} %copy-done), kind=kOutput, calls=%fused_computation.31 | convolution fusion | flops 536936448 | bytes 4325376 | tf_op jit(solution)/shard_map/dot_general | solution.py:99
  194.1 0.3 copy-done.5
  194.4 0.8 convolution_convert_fusion.2
  195.2 5.8 %convolution_convert_fusion = bf16[256,1024]{1,0:T(8,128)(2,1)S(1)} fusion(bf16[256,4096]{0,1:T(8,128)(2,1)S(1)} %bitcast.102, bf16[4096,1024]{1,0:T(8,128)(2,1)} %param.25), kind=kOutput, calls=%fused_computation.30 | convolution fusion | flops 2147745792 | bytes 11010048 | tf_op jit(solution)/shard_map/dot_general | solution.py:96
  201.0 1.2 reshape.202
  202.2 7.1 %all_gather.27 = bf16[1024,256]{1,0:T(8,128)(2,1)S(1)} all-gather(bf16[256,256]{1,0:T(8,128)(2,1)S(1)} %convolution_convert_fusion.2), channel_id=1, replica_groups=mesh['doc'=2,'seq'=4,'head'=4] {'seq'}, dimensions={0}, use_global_device_ids=true | all-gather | bytes 655360 | tf_op jit(solution)/shard_map/all_gather | solution.py:107
  209.3 0.2 copy.46
  209.5 7.5 %all_gather.28 = bf16[1024,256]{1,0:T(8,128)(2,1)S(1)} all-gather(bf16[256,256]{1,0:T(8,128)(2,1)S(1)} %convolution_convert_fusion.1), channel_id=1, replica_groups=mesh['doc'=2,'seq'=4,'head'=4] {'seq'}, dimensions={0}, use_global_device_ids=true | all-gather | bytes 655360 | tf_op jit(solution)/shard_map/all_gather | solution.py:106
  217.0 0.9 reshape.201
  217.9 2.7 %fusion.1 = (f32[256,2,4]{0,2,1:T(4,128)S(1)}, f32[2,1024,256,4]{2,1,3,0:T(8,128)S(1)}) fusion(pred[256,1024]{0,1:T(8,128)(4,1)S(1)} %fusion.34, bf16[256,2,4,128]{3,2,1,0:T(4,128)(2,1)} %reshape.202, bf16[1024,2,128,1]{2,1,0,3:T(2,128)(2,1)} %bitcast.111), kind=kOutput, calls=%fused_computation.5 | convolution fusion | flops 543160320 | bytes 9707520 | tf_op jit(solution)/shard_map/tkgd,rkd->tkgr/dot_general | solution.py:111
  220.6 2.0 fusion.2
  222.6 3.2 %fusion.11 = f32[2,128,256,4]{2,1,3,0:T(8,128)} fusion(bf16[1024,2,128,1]{0,2,3,1:T(8,128)(2,1)S(1)} %bitcast.110, f32[2,1024,256,4]{2,1,3,0:T(8,128)S(1)} %get-tuple-element.138, f32[256,2,4]{0,2,1:T(4,128)S(1)} %broadcast_maximum_fusion, pred[256,1024]{0,1:T(8,128)(4,1)S(1)} %fusion.34), kind=kOutput, calls=%fused_computation.15 | convolution fusion | flops 547356672 | bytes 10231808 | tf_op jit(solution)/shard_map/tkgr,rkd->tkgd/dot_general | solution.py:123
  225.9 1.6 copy.42
  227.5 0.1 copy.41
  227.6 0.3 div.27
  227.9 1.0 fusion.30
  (34 shorter events, 0.4 us)
Async XLA Ops:
  7.2 184.4 %copy-start = (bf16[4096,256]{1,0:T(8,128)(2,1)S(1)}, bf16[4096,256]{1,0:T(8,128)(2,1)}, u32[]{:S(2)}) copy-start(bf16[4096,256]{1,0:T(8,128)(2,1)} %param.26) | copy-start | bytes 6291460
  7.2 32.4 %all-gather.6.cloned.1.call-start = ((), (), s32[]{:S(2)}) async-start(), calls=%async_computation.2 | async-start | bytes 2621440 | tf_op jit(solution)/shard_map/all_gather | solution.py:14
  14.2 115.8 %reduce-scatter.2.cloned.1.call-start = ((), (), s32[]{:S(2)}) async-start(), calls=%async_computation.1 | async-start | bytes 5242880 | tf_op jit(solution)/shard_map/reduce_scatter | solution.py:87
  31.1 12.2 %copy-start.4 = (bf16[256,128]{1,0:T(8,128)(2,1)S(1)}, bf16[256,128]{1,0:T(8,128)(2,1)}, u32[]{:S(2)}) copy-start(bf16[256,128]{1,0:T(8,128)(2,1)} %param.19) | copy-start | bytes 196612
  53.0 77.0 %copy-start.3 = (bf16[256,1024]{1,0:T(8,128)(2,1)S(1)}, bf16[256,1024]{1,0:T(8,128)(2,1)}, u32[]{:S(2)}) copy-start(bf16[256,1024]{1,0:T(8,128)(2,1)} %param.16) | copy-start | bytes 1572868
  53.1 134.6 %all-gather.8.cloned.1.call-start = ((), (), s32[]{:S(2)}) async-start(), calls=%async_computation.3 | async-start | bytes 2621440 | tf_op jit(solution)/shard_map/all_gather | solution.py:95
  131.5 62.6 %copy-start.2 = (bf16[256,1024]{1,0:T(8,128)(2,1)}, bf16[256,1024]{1,0:T(8,128)(2,1)S(1)}, u32[]{:S(2)}) copy-start(bf16[256,1024]{1,0:T(8,128)(2,1)S(1)} %get-tuple-element.128) | copy-start | bytes 1572868
  191.6 2.5 %copy-start.1 = (bf16[4,256,1024]{1,2,0:T(8,128)(2,1)S(1)}, bf16[4,256,1024]{1,2,0:T(8,128)(2,1)}, u32[]{:S(2)}) copy-start(bf16[4,256,1024]{1,2,0:T(8,128)(2,1)} %copy.36) | copy-start | bytes 6291460
  191.6 2.9 %copy-start.5 = (bf16[4096,256]{1,0:T(8,128)(2,1)S(1)}, bf16[4096,256]{1,0:T(8,128)(2,1)}, u32[]{:S(2)}) copy-start(bf16[4096,256]{1,0:T(8,128)(2,1)} %param.27) | copy-start | bytes 6291460
Sparse Core Ops, SparseCore 0:
  14.3 25.2 all-gather.5
  53.2 76.7 reduce-scatter.1
  143.6 43.9 all-gather.7
